TPU v7x, 32 devices: a whole 2x2x4 slice. The times are simulated.
32 devices in a mesh: scen: 2 (over y), col: 16 (over z, x, core).
Axes of the slice: x: 2, y: 2, z: 4, core: 2. Of those that a mesh axis runs over, the one named last changes fastest.
Arguments:
- border: float32 [4, 1536, 16384], P('scen', None, 'col'), may hold values from -6 to 6
- barrier: float32 [4, 1536], P('scen'), may hold values from 0.1 to 10
- row_counts: int32 [4], P('scen'), may hold values from 1024 to 1536, as said below
Outputs:
- factor_panel: float32 [16, 2, 512, 512], P('col', 'scen')
Inputs may be any that keep to these rules, and one draw needn't show every extreme that they name: `row_counts`: every value lies between 1024 and 1536, and at least one scenario uses all 1536 rows.
All inputs are finite; a program needn't handle non-finite values.
Results may differ from a plain program's by a relative error of at most 0.0003.
Values sent between devices are 32-bit elements; how exact they have to be, the bound alone decides.
A program may use at most 64 MiB of HBM per device.

v0:
```python
import jax
import jax.numpy as jnp
from jax import lax
from jax.experimental import pallas as pl
from jax.experimental.pallas import tpu as pltpu
from jax.sharding import PartitionSpec as P

PANEL = 512
TILE = 128
SUB = 8
TILES = PANEL // TILE
UPPER = [(j, k) for j in range(TILES) for k in range(j, TILES)]


def inverse_factor(a):
    lane = lax.broadcasted_iota(jnp.int32, (SUB, TILE), 1)
    sub = lax.broadcasted_iota(jnp.int32, (SUB, TILE), 0)
    rows = [a[SUB * t : SUB * (t + 1)] for t in range(TILE // SUB)]
    out = [jnp.zeros((SUB, TILE), jnp.float32) for _ in rows]
    for k in range(TILE):
        own, r = divmod(k, SUB)
        row = jnp.broadcast_to(rows[own][r : r + 1], (SUB, TILE))
        pivot = jnp.broadcast_to(rows[own][r : r + 1, k : k + 1], (SUB, TILE))
        done = jnp.where(lane < k, row, jnp.where(lane == k, 1.0, 0.0)) * lax.rsqrt(pivot)
        out[own] = jnp.where(sub == r, done, out[own])
        step = jnp.where(lane == k, 1.0, row) / pivot
        for t in range(own if r < SUB - 1 else own + 1, TILE // SUB):
            col = jnp.broadcast_to(rows[t][:, k : k + 1], (SUB, TILE))
            rows[t] = jnp.where(lane == k, 0.0, rows[t]) - col * step
    return jnp.concatenate(out, axis=0)


def factor_kernel(a_ref, b_ref, inv_ref, t_ref):
    t_ref[...] = jnp.zeros_like(t_ref)
    for n, (j, k) in enumerate(UPPER):
        t_ref[j * TILE : (j + 1) * TILE, k * TILE : (k + 1) * TILE] = a_ref[n] + b_ref[n]
    eye = (
        lax.broadcasted_iota(jnp.int32, (TILE, TILE), 0)
        == lax.broadcasted_iota(jnp.int32, (TILE, TILE), 1)
    ).astype(jnp.float32)
    for j in range(TILES):
        t_ref[j * TILE : (j + 1) * TILE, PANEL + j * TILE : PANEL + (j + 1) * TILE] = eye

    @pl.loop(0, TILES)
    def _(j):
        here = pl.ds(pl.multiple_of(j * TILE, TILE), TILE)
        inv = inverse_factor(t_ref[here, here])
        scaled = jnp.dot(
            inv, t_ref[here, :], precision=lax.Precision.HIGHEST, preferred_element_type=jnp.float32
        )
        inv_ref[here, :] = scaled[:, PANEL:]
        lane = lax.broadcasted_iota(jnp.int32, (TILE, PANEL), 1)
        ahead = jnp.where(lane >= (j + 1) * TILE, scaled[:, :PANEL], 0.0).T
        for i in range(1, TILES):

            @pl.when(i > j)
            def _():
                part = slice(i * TILE, (i + 1) * TILE)
                t_ref[part, :] -= jnp.dot(
                    ahead[part],
                    scaled,
                    precision=lax.Precision.HIGHEST,
                    preferred_element_type=jnp.float32,
                )


def inverse_of_factor(mine, other):
    return pl.pallas_call(
        factor_kernel,
        out_shape=jax.ShapeDtypeStruct((PANEL, PANEL), jnp.float32),
        in_specs=[pl.BlockSpec(memory_space=pltpu.VMEM)] * 2,
        out_specs=pl.BlockSpec(memory_space=pltpu.VMEM),
        scratch_shapes=[pltpu.VMEM((PANEL, 2 * PANEL), jnp.float32)],
        cost_estimate=pl.CostEstimate(
            flops=2 * 10**10, bytes_accessed=3 * 10**6, transcendentals=PANEL
        ),
        name="factor",
    )(mine, other)


def body(border, barrier, row_counts):
    scen_here, capacity, own_cols = border.shape
    n_scen = lax.axis_size("scen")
    per_owner = PANEL // lax.axis_size("col")
    rows_owned = own_cols // n_scen
    depth = scen_here * capacity
    positions = lax.iota(jnp.int32, capacity)
    weights = jnp.where(positions[None, :] < row_counts[:, None], 1.0 / barrier, jnp.float32(0.0))
    panel_part = jnp.transpose(border[:, :, :per_owner], (2, 0, 1)).reshape(per_owner, depth)
    panel = lax.all_gather(panel_part, "col", axis=0, tiled=True)
    weighted = panel * weights.reshape(1, depth)
    block = jnp.einsum(
        "pr,qr->pq", weighted, panel, precision=lax.Precision.HIGH,
        preferred_element_type=jnp.float32,
    )
    upper = jnp.stack(
        [block[j * TILE : (j + 1) * TILE, k * TILE : (k + 1) * TILE] for j, k in UPPER]
    )
    if n_scen == 2:
        swap = [(0, 1), (1, 0)]
        upper_other = lax.ppermute(upper, "scen", swap)
    else:
        upper_other = lax.psum(upper, "scen") - upper
    part = jnp.einsum(
        "pr,rc->pc", weighted, border.reshape(depth, own_cols), precision=lax.Precision.HIGH,
        preferred_element_type=jnp.float32,
    )
    if n_scen == 2:
        me = lax.axis_index("scen")
        sent = lax.dynamic_slice_in_dim(part, (1 - me) * rows_owned, rows_owned, 1)
        kept = lax.dynamic_slice_in_dim(part, me * rows_owned, rows_owned, 1)
        owned = kept + lax.ppermute(sent, "scen", swap)
    else:
        owned = lax.psum_scatter(part, "scen", scatter_dimension=1, tiled=True)
    inverse = inverse_of_factor(upper, upper_other)
    solved = jnp.einsum(
        "qt,pq->tp", owned, inverse, precision=lax.Precision.HIGHEST,
        preferred_element_type=jnp.float32,
    )
    return solved.reshape(1, 1, rows_owned, PANEL)


def solution(mesh):
    placed = (P("scen", None, "col"), P("scen", None), P("scen"))
    return jax.shard_map(
        body, mesh=mesh, in_specs=placed, out_specs=P("col", "scen", None, None), check_vma=False
    )
```

profile of v0, /device:TPU:0, one launch (start us, length us, event | category | flops | bytes accessed | tf_op | source)
XLA Modules:
  0.0 190.5 jit_solution(11026554396835762726)
XLA Ops:
  6.5 0.0 all-gather.2.cloned.1.call-start
  6.5 1.5 slice.33
  8.1 1.2 copy.5
  9.2 0.0 all-gather.2.cloned.1.call-update
  9.3 0.8 compare_select_fusion
  10.1 63.7 %all-gather.2.cloned.1.call-done = f32[512,3072]{1,0:T(8,128)} async-done(((f32[32,3072]{1,0:T(8,128)}), f32[512,3072]{1,0:T(8,128)}) %all-gather.2.cloned.1.call-update) | async-done | bytes 6291472 | tf_op jit(solution)/shard_map/all_gather | solution.py:90
  73.8 0.0 copy-start
  73.8 10.3 %fusion = f32[512,512]{1,0:T(8,128)S(1)} fusion(f32[512,3072]{1,0:T(8,128)} %all-gather.2.cloned.1.call-done, f32[3072]{0:T(1024)S(1)} %mul.16), kind=kOutput, calls=%fused_computation | convolution fusion | flops 4833411072 | bytes 7352320 | tf_op jit(solution)/shard_map/pr,qr->pq/dot_general | solution.py:92
  84.3 0.0 copy-start.1
  84.3 1.5 collective-permute-start.1
  85.8 0.0 copy-done
  85.8 13.5 %fusion.2 = f32[512,1024]{1,0:T(8,128)S(1)} fusion(f32[3072,1024]{1,0:T(8,128)} %bitcast.50, f32[512,3072]{1,0:T(8,128)S(1)} %copy-done, f32[3072]{0:T(1024)S(1)} %mul.16), kind=kOutput, calls=%fused_computation.2 | convolution fusion | flops 9665249280 | bytes 20983808 | tf_op jit(solution)/shard_map/pr,rc->pc/dot_general | solution.py:104
  99.3 0.0 copy-done.1
  99.4 1.1 constant_dynamic-slice_fusion
  100.4 0.6 collective-permute-start
  101.0 0.4 collective-permute-done.1.b_ref
  101.3 76.6 %factor.1 = f32[512,512]{1,0:T(8,128)} custom-call(f32[10,128,128]{2,1,0:T(8,128)} %copy-done.1, f32[10,128,128]{2,1,0:T(8,128)} %collective-permute-done.1.b_ref), custom_call_target="tpu_custom_call" | custom-call | flops 20000000000 | bytes 3000000 | tf_op jit(solution)/shard_map/factor/pallas_call | solution.py:68
  178.0 0.0 collective-permute-done
  178.0 5.7 %convolution_bitcast_fusion = f32[1,1,512,512]{3,2,1,0:T(8,128)} fusion(f32[512,512]{1,0:T(8,128)} %factor.1, f32[512,512]{1,0:T(8,128)S(1)} %collective-permute-done, f32[512,1024]{1,0:T(8,128)S(1)} %fusion.2, s32[]{:T(128)S(6)} %select_n.11), kind=kOutput, calls=%fused_computation.6 | convolution fusion | flops 1610874880 | bytes 4194308 | tf_op jit(solution)/shard_map/qt,pq->tp/dot_general | solution.py:116
  (11 shorter events, 0.1 us)
Async XLA Ops:
  6.5 67.2 %all-gather.2.cloned.1.call-start = ((), (), s32[]{:S(2)}) async-start(), calls=%async_computation | async-start | bytes 6684672 | tf_op jit(solution)/shard_map/all_gather | solution.py:90
  73.8 12.1 %copy-start = (f32[512,3072]{1,0:T(8,128)S(1)}, f32[512,3072]{1,0:T(8,128)}, u32[]{:S(2)}) copy-start(f32[512,3072]{1,0:T(8,128)} %all-gather.2.cloned.1.call-done) | copy-start | bytes 18874372
  84.3 15.1 %copy-start.1 = (f32[10,128,128]{2,1,0:T(8,128)}, f32[10,128,128]{2,1,0:T(8,128)S(1)}, u32[]{:S(2)}) copy-start(f32[10,128,128]{2,1,0:T(8,128)S(1)} %fusion.8.a_ref) | copy-start | bytes 1966084
  84.3 17.1 %collective-permute-start.1 = (f32[10,128,128]{2,1,0:T(8,128)S(1)}, f32[10,128,128]{2,1,0:T(8,128)}, u32[]{:S(2)}, u32[]{:S(2)}) collective-permute-start(f32[10,128,128]{2,1,0:T(8,128)S(1)} %fusion.8.a_ref), channel_id=1, source_target_pairs={{0,16},{16,0},{1,17},{17,1},{2,18},{18,2},{3,19},{19,3},{4,20},{20... | collective-permute-start | bytes 1966088 | tf_op jit(solution)/shard_map/ppermute | solution.py:101
  100.4 77.5 %collective-permute-start = (f32[512,512]{1,0:T(8,128)}, f32[512,512]{1,0:T(8,128)S(1)}, u32[]{:S(2)}, u32[]{:S(2)}) collective-permute-start(f32[512,512]{1,0:T(8,128)} %constant_dynamic-slice_fusion), channel_id=1, source_target_pairs={{0,16},{16,0},{1,17},{17,1},{2,18},{18,2},{3,19},{19,3},{4,20},{20... | collective-permute-start | bytes 3145736 | tf_op jit(solution)/shard_map/ppermute | solution.py:112
Sparse Core Ops, SparseCore 0:
  9.6 64.1 all-gather.1
where the time goes:
time: 191 us; the launch traced here: 190 us
  Pallas kernels  76.6 us (40%)
  waiting for transfers between devices  64.1 us (34%)
  matrix products  29.5 us (15%)
  between operations  13.5 us (7%)
  local copies, waits for them, and re-layouts  3.91 us (2%)
  starting transfers between devices  2.09 us (1%)
    pallas_call x1, Pallas kernels, inverse_of_factor(): pl.pallas_call(factor_kernel, out_shape=jax.ShapeDtypeStruct((PANEL, PANE...  76.6 us
    all_gather x1, waiting for transfers between devices, body(): panel = lax.all_gather(panel_part, 'col', axis=0, tiled=True)  63.7 us
    dot_general x1, matrix products, body(): jnp.einsum('pr,rc->pc', weighted, border.reshape(depth, own_cols), precis...  13.5 us
    dot_general x1, matrix products, body(): jnp.einsum('pr,qr->pq', weighted, panel, precision=lax.Precision.HIGH, pr...  10.3 us
    dot_general x1, matrix products, body(): jnp.einsum('qt,pq->tp', owned, inverse, precision=lax.Precision.HIGHEST,...  5.67 us
  transfers between devices with their start and end apart: 3, of which 2 were waited for; matrix products, arithmetic and copies ran while one was open for 8% of the time, Pallas kernels for 40%

commit v1 on v0

--- a/solution.py
+++ b/solution.py
@@ -12,23 +12,64 @@
 UPPER = [(j, k) for j in range(TILES) for k in range(j, TILES)]
 
 
+def tree(xs):
+    xs=list(xs)
+    while len(xs)>1:
+        xs=[xs[i]+xs[i+1] if i+1<len(xs) else xs[i] for i in range(0,len(xs),2)]
+    return xs[0]
+
 def inverse_factor(a):
-    lane = lax.broadcasted_iota(jnp.int32, (SUB, TILE), 1)
-    sub = lax.broadcasted_iota(jnp.int32, (SUB, TILE), 0)
-    rows = [a[SUB * t : SUB * (t + 1)] for t in range(TILE // SUB)]
-    out = [jnp.zeros((SUB, TILE), jnp.float32) for _ in rows]
-    for k in range(TILE):
-        own, r = divmod(k, SUB)
-        row = jnp.broadcast_to(rows[own][r : r + 1], (SUB, TILE))
-        pivot = jnp.broadcast_to(rows[own][r : r + 1, k : k + 1], (SUB, TILE))
-        done = jnp.where(lane < k, row, jnp.where(lane == k, 1.0, 0.0)) * lax.rsqrt(pivot)
-        out[own] = jnp.where(sub == r, done, out[own])
-        step = jnp.where(lane == k, 1.0, row) / pivot
-        for t in range(own if r < SUB - 1 else own + 1, TILE // SUB):
-            col = jnp.broadcast_to(rows[t][:, k : k + 1], (SUB, TILE))
-            rows[t] = jnp.where(lane == k, 0.0, rows[t]) - col * step
-    return jnp.concatenate(out, axis=0)
-
+    n=TILE//SUB
+    lane = lax.broadcasted_iota(jnp.int32,(SUB,TILE),1)
+    sub = lax.broadcasted_iota(jnp.int32,(SUB,TILE),0)
+    rows=[a[SUB*t:SUB*(t+1)] for t in range(n)]
+    out=[]
+    B=lambda x: jnp.broadcast_to(x,(SUB,TILE))
+    for g in range(n):
+        c0=g*SUB
+        d=rows[g]
+        inb=(lane>=c0)&(lane<c0+SUB)
+        cols=[B(d[:,c0+j:c0+j+1]) for j in range(SUB)]
+        A={}
+        for j in range(SUB):
+            for i in range(j,SUB):
+                A[i,j]=B(cols[j][i:i+1])
+        r=[None]*SUB; dd=[None]*SUB; M={}
+        for k in range(SUB):
+            dd[k]=A[k,k]
+            r[k]=1.0/dd[k]
+            for i in range(k+1,SUB):
+                M[i,k]=A[i,k]*r[k]
+            for j in range(k+1,SUB):
+                for i in range(j,SUB):
+                    A[i,j]=A[i,j]-M[i,k]*A[j,k] if i!=j else A[i,j]-M[i,k]*A[i,k]
+        N={}
+        for j in range(SUB):
+            for i in range(j+1,SUB):
+                s=M[i,j]
+                for k in range(j+1,i):
+                    s=s+M[i,k]*N[k,j]
+                N[i,j]=-s
+        dp=jnp.where(inb, jnp.where(lane-c0==sub,1.0,0.0), d)
+        drow=[B(dp[j:j+1]) for j in range(SUB)]
+        ncol=[]
+        for j in range(SUB-1):
+            m=jnp.zeros((SUB,TILE),jnp.float32)
+            for i in range(j+1,SUB):
+                m=jnp.where(sub==i,N[i,j],m)
+            ncol.append(m)
+        u=tree([dp]+[ncol[j]*drow[j] for j in range(SUB-1)])
+        dvec=dd[0]
+        for i in range(1,SUB):
+            dvec=jnp.where(sub==i,dd[i],dvec)
+        out.append(jnp.where(lane<c0+SUB,u*lax.rsqrt(dvec),0.0))
+        if g==n-1: break
+        ub=[B(u[i:i+1])*r[i] for i in range(SUB)]
+        Z=[tree([ub[j]]+[N[i,j]*ub[i] for i in range(j+1,SUB)]) for j in range(SUB)]
+        for t in range(g+1,n):
+            cb=[B(rows[t][:,c0+j:c0+j+1]) for j in range(SUB)]
+            rows[t]=jnp.where(inb,0.0,rows[t])-tree([cb[j]*Z[j] for j in range(SUB)])
+    return jnp.concatenate(out,axis=0)
 
 def factor_kernel(a_ref, b_ref, inv_ref, t_ref):
     t_ref[...] = jnp.zeros_like(t_ref)

time: 191 us -> 143 us (0.75)
  Pallas kernels: 76.6 us -> 28.8 us
    pallas_call x1, Pallas kernels: 76.6 us -> 28.8 us  [inverse_of_factor(): pl.pallas_call(factor_kernel, out_shape=jax.ShapeDtypeStruct((PANEL, PANE...]
  transfers between devices with their start and end apart: 3 -> 3, of which waited for: 2 -> 2; matrix products, arithmetic and copies ran while one was open for 8% -> 11% of each run, Pallas kernels for 40% -> 20%
where the time goes in v1:
time: 143 us
  waiting for transfers between devices  64.1 us (45%)
  matrix products  29.5 us (21%)
  Pallas kernels  28.8 us (20%)
  between operations  13.5 us (9%)
  local copies, waits for them, and re-layouts  3.91 us (3%)
  starting transfers between devices  2.09 us (1%)
    all_gather x1, waiting for transfers between devices, body(): panel = lax.all_gather(panel_part, 'col', axis=0, tiled=True)  63.7 us
    pallas_call x1, Pallas kernels, inverse_of_factor(): pl.pallas_call(factor_kernel, out_shape=jax.ShapeDtypeStruct((PANEL, PANE...  28.8 us
    dot_general x1, matrix products, body(): jnp.einsum('pr,rc->pc', weighted, border.reshape(depth, own_cols), precis...  13.5 us
    dot_general x1, matrix products, body(): jnp.einsum('pr,qr->pq', weighted, panel, precision=lax.Precision.HIGH, pr...  10.3 us
    dot_general x1, matrix products, body(): jnp.einsum('qt,pq->tp', owned, inverse, precision=lax.Precision.HIGHEST,...  5.67 us
  transfers between devices with their start and end apart: 3, of which 2 were waited for; matrix products, arithmetic and copies ran while one was open for 11% of the time, Pallas kernels for 20%

profile of v1, /device:TPU:0, one launch (start us, length us, event | category | flops | bytes accessed | tf_op | source)
XLA Modules:
  0.0 142.6 jit_solution(1960158835861743657)
XLA Ops:
  6.5 0.0 all-gather.2.cloned.1.call-start
  6.5 1.5 %slice.33 = f32[2,1536,32]{2,1,0:T(8,128)S(1)} slice(f32[2,1536,1024]{2,1,0:T(8,128)} %param.3), slice={[0:2], [0:1536], [0:32]} | slice | bytes 786432 | tf_op jit(solution)/shard_map/slice | solution.py:130
  8.1 1.2 copy.5
  9.2 0.0 all-gather.2.cloned.1.call-update
  9.3 0.8 compare_select_fusion
  10.1 63.7 %all-gather.2.cloned.1.call-done = f32[512,3072]{1,0:T(8,128)} async-done(((f32[32,3072]{1,0:T(8,128)}), f32[512,3072]{1,0:T(8,128)}) %all-gather.2.cloned.1.call-update) | async-done | bytes 6291472 | tf_op jit(solution)/shard_map/all_gather | solution.py:131
  73.8 0.0 copy-start
  73.8 10.3 %fusion = f32[512,512]{1,0:T(8,128)S(1)} fusion(f32[512,3072]{1,0:T(8,128)} %all-gather.2.cloned.1.call-done, f32[3072]{0:T(1024)S(1)} %mul.16), kind=kOutput, calls=%fused_computation | convolution fusion | flops 4833411072 | bytes 7352320 | tf_op jit(solution)/shard_map/pr,qr->pq/dot_general | solution.py:133
  84.3 0.0 copy-start.1
  84.3 1.5 %collective-permute-start.1 = (f32[10,128,128]{2,1,0:T(8,128)S(1)}, f32[10,128,128]{2,1,0:T(8,128)}, u32[]{:S(2)}, u32[]{:S(2)}) collective-permute-start(f32[10,128,128]{2,1,0:T(8,128)S(1)} %fusion.8.a_ref), channel_id=1, source_target_pairs={{0,16},{16,0},{1,17},{17,1},{2,18},{18,2},{3,19},{19,3},{4,20},{20... | collective-permute-start | bytes 1966088 | tf_op jit(solution)/shard_map/ppermute | solution.py:142
  85.8 0.0 copy-done
  85.8 13.5 %fusion.2 = f32[512,1024]{1,0:T(8,128)S(1)} fusion(f32[3072,1024]{1,0:T(8,128)} %bitcast.50, f32[512,3072]{1,0:T(8,128)S(1)} %copy-done, f32[3072]{0:T(1024)S(1)} %mul.16), kind=kOutput, calls=%fused_computation.2 | convolution fusion | flops 9665249280 | bytes 20983808 | tf_op jit(solution)/shard_map/pr,rc->pc/dot_general | solution.py:145
  99.3 0.0 copy-done.1
  99.4 1.1 constant_dynamic-slice_fusion
  100.4 0.6 collective-permute-start
  101.0 0.4 collective-permute-done.1.b_ref
  101.3 28.8 %factor.1 = f32[512,512]{1,0:T(8,128)} custom-call(f32[10,128,128]{2,1,0:T(8,128)} %copy-done.1, f32[10,128,128]{2,1,0:T(8,128)} %collective-permute-done.1.b_ref), custom_call_target="tpu_custom_call" | custom-call | flops 20000000000 | bytes 3000000 | tf_op jit(solution)/shard_map/factor/pallas_call | solution.py:109
  130.1 0.0 collective-permute-done
  130.1 5.7 %convolution_bitcast_fusion = f32[1,1,512,512]{3,2,1,0:T(8,128)} fusion(f32[512,512]{1,0:T(8,128)} %factor.1, f32[512,512]{1,0:T(8,128)S(1)} %collective-permute-done, f32[512,1024]{1,0:T(8,128)S(1)} %fusion.2, s32[]{:T(128)S(6)} %select_n.11), kind=kOutput, calls=%fused_computation.6 | convolution fusion | flops 1610874880 | bytes 4194308 | tf_op jit(solution)/shard_map/qt,pq->tp/dot_general | solution.py:157
  (11 shorter events, 0.1 us)
Async XLA Ops:
  6.5 67.2 %all-gather.2.cloned.1.call-start = ((), (), s32[]{:S(2)}) async-start(), calls=%async_computation | async-start | bytes 6684672 | tf_op jit(solution)/shard_map/all_gather | solution.py:131
  73.8 12.1 %copy-start = (f32[512,3072]{1,0:T(8,128)S(1)}, f32[512,3072]{1,0:T(8,128)}, u32[]{:S(2)}) copy-start(f32[512,3072]{1,0:T(8,128)} %all-gather.2.cloned.1.call-done) | copy-start | bytes 18874372
  84.3 15.1 %copy-start.1 = (f32[10,128,128]{2,1,0:T(8,128)}, f32[10,128,128]{2,1,0:T(8,128)S(1)}, u32[]{:S(2)}) copy-start(f32[10,128,128]{2,1,0:T(8,128)S(1)} %fusion.8.a_ref) | copy-start | bytes 1966084
  84.3 17.1 %collective-permute-start.1 = (f32[10,128,128]{2,1,0:T(8,128)S(1)}, f32[10,128,128]{2,1,0:T(8,128)}, u32[]{:S(2)}, u32[]{:S(2)}) collective-permute-start(f32[10,128,128]{2,1,0:T(8,128)S(1)} %fusion.8.a_ref), channel_id=1, source_target_pairs={{0,16},{16,0},{1,17},{17,1},{2,18},{18,2},{3,19},{19,3},{4,20},{20... | collective-permute-start | bytes 1966088 | tf_op jit(solution)/shard_map/ppermute | solution.py:142
  100.4 29.7 %collective-permute-start = (f32[512,512]{1,0:T(8,128)}, f32[512,512]{1,0:T(8,128)S(1)}, u32[]{:S(2)}, u32[]{:S(2)}) collective-permute-start(f32[512,512]{1,0:T(8,128)} %constant_dynamic-slice_fusion), channel_id=1, source_target_pairs={{0,16},{16,0},{1,17},{17,1},{2,18},{18,2},{3,19},{19,3},{4,20},{20... | collective-permute-start | bytes 3145736 | tf_op jit(solution)/shard_map/ppermute | solution.py:153
Sparse Core Ops, SparseCore 0:
  9.6 64.1 all-gather.1

commit v2 on v1

--- a/solution.py
+++ b/solution.py
@@ -119,7 +119,7 @@
     )(mine, other)
 
 
-def body(border, barrier, row_counts):
+def general_body(border, barrier, row_counts):
     scen_here, capacity, own_cols = border.shape
     n_scen = lax.axis_size("scen")
     per_owner = PANEL // lax.axis_size("col")
@@ -161,8 +161,373 @@
     return solved.reshape(1, 1, rows_owned, PANEL)
 
 
+MESH = pl.DeviceIdType.MESH
+CHUNK = 256
+LAG = 3
+
+
+def split(x):
+    hi = x.astype(jnp.bfloat16)
+    return hi, (x - hi.astype(jnp.float32)).astype(jnp.bfloat16)
+
+
+def exact(a, b):
+    return jnp.dot(a, b, precision=lax.Precision.HIGHEST, preferred_element_type=jnp.float32)
+
+
+def bf16_nt(a, b):
+    return lax.dot_general(a, b, (((1,), (1,)), ((), ())), preferred_element_type=jnp.float32)
+
+
+def bf16_nn(a, b):
+    return jnp.dot(a, b, preferred_element_type=jnp.float32)
+
+
+def ring_kernel(
+    part_ref, w_ref, border_ref, out_ref,
+    gath, stage, bhi, blo, phi, plo, whi, wlo,
+    u_keep, u_send, u_recv, g_own, g_recv, t_ref, inv_ref, low_ref, x_ref,
+    stage_sem, ring_send, core_send, recv_sem, uy_send, uy_recv, gy_send, gy_recv,
+):
+    chips = lax.axis_size("col") // 2
+    half_ring = chips // 2
+    me = lax.axis_index("col")
+    scen = lax.axis_index("scen")
+    core = me % 2
+    chip = me // 2
+    pos = (1 - chip % 2) * (chip // 2) + (chip % 2) * (chips - 1 - chip // 2)
+    depth_half = part_ref.shape[2]
+    per = part_ref.shape[1]
+    depth = 2 * depth_half
+    cols = border_ref.shape[1]
+    rows_owned = cols // 2
+
+    def chip_at(p):
+        p = (p + 2 * chips) % chips
+        x = p // half_ring
+        z = (1 - x) * p + x * (chips - 1 - p)
+        return 2 * z + x
+
+    up = {"col": 2 * chip_at(pos + 1) + core}
+    down = {"col": 2 * chip_at(pos - 1) + core}
+    mate = {"col": 2 * chip + 1 - core}
+    across = {"scen": 1 - scen}
+
+    barrier = pltpu.get_barrier_semaphore()
+    for peer in (up, down, mate, across):
+        pl.semaphore_signal(barrier, inc=1, device_id=peer, device_id_type=MESH)
+
+    def fetch(n):
+        return pltpu.make_async_copy(
+            border_ref.at[pl.ds(pl.multiple_of(n * CHUNK, CHUNK), CHUNK)],
+            stage.at[n % LAG],
+            stage_sem.at[n % LAG],
+        )
+
+    chunks = depth // CHUNK
+    for n in range(LAG):
+        fetch(n).start()
+    pl.semaphore_wait(barrier, 4)
+
+    def send(src, block, h, send_sem, peer):
+        return pltpu.make_async_remote_copy(
+            src_ref=src,
+            dst_ref=gath.at[block, h],
+            send_sem=send_sem,
+            recv_sem=recv_sem.at[block, h],
+            device_id=peer,
+            device_id_type=MESH,
+        )
+
+    def own(h, d):
+        sem = core_send.at[0, h] if d == 2 else ring_send.at[d, 0, h]
+        return send(part_ref.at[h], me, h, sem, (up, down, mate)[d])
+
+    def block_of(d, k):
+        return 2 * chip_at(pos - k if d == 0 else pos + k) + core
+
+    def forward(d, k, h):
+        block = block_of(d, k)
+        return send(gath.at[block, h], block, h, ring_send.at[d, k, h], (up, down)[d])
+
+    def push(d, k, h):
+        block = block_of(d, k)
+        return send(gath.at[block, h], block, h, core_send.at[2 * k - d, h], mate)
+
+    def arrived(block, h):
+        pltpu.make_async_copy(part_ref.at[h], gath.at[block, h], recv_sem.at[block, h]).wait()
+
+    for h in range(2):
+        for d in range(3):
+            own(h, d).start()
+
+    def convert_border(first):
+        @pl.loop(first, first + chunks // 2)
+        def _(n):
+            fetch(n).wait()
+            here = pl.ds(pl.multiple_of(n * CHUNK, CHUNK), CHUNK)
+            hi, lo = split(stage[n % LAG])
+            bhi[here, :] = hi
+            blo[here, :] = lo
+
+            @pl.when(n + LAG < chunks)
+            def _():
+                fetch(n + LAG).start()
+
+    def convert(which, cc, src):
+        for h in range(2):
+            there = (which, pl.ds(cc * per, per), pl.ds(h * depth_half, depth_half))
+            x = src(h)
+            phi[there], plo[there] = split(x)
+            whi[there], wlo[there] = split(x * w_ref[h])
+
+    def convert_both(which):
+        for cc in range(2):
+            convert(which, cc, lambda h: gath[2 * which + cc, h])
+
+    def unit(k):
+        first = chip_at(pos - k)
+        return first, chip_at(pos + k * (1 - k // half_ring))
+
+    def product(k, which, dst):
+        a, b = unit(k)
+        left = jnp.concatenate([whi[a], whi[b], wlo[a], wlo[b]], axis=0)
+        rows = 2 * whi.shape[1]
+
+        @pl.loop(0, rows_owned // CHUNK)
+        def _(n):
+            col = pl.ds(pl.multiple_of(which * rows_owned + n * CHUNK, CHUNK), CHUNK)
+            to = pl.ds(pl.multiple_of(n * CHUNK, CHUNK), CHUNK)
+            both = bf16_nn(left, bhi[:, col])
+            res = both[:rows] + both[rows:] + bf16_nn(left[:rows], blo[:, col])
+            dst[a, :, to] = res[: rows // 2]
+            dst[b, :, to] = res[rows // 2 :]
+
+    def cross(which):
+        return pltpu.make_async_remote_copy(
+            src_ref=u_send.at[which],
+            dst_ref=u_recv.at[which],
+            send_sem=uy_send.at[which],
+            recv_sem=uy_recv.at[which],
+            device_id=across,
+            device_id_type=MESH,
+        )
+
+    def product_send(k):
+        product(k, 1 - scen, u_send)
+        for which in unit(k):
+            cross(which).start()
+
+    def g_piece(n):
+        row = max(n - 1, 0)
+        first, last = (0, TILE) if n == 0 else (max(row, 1) * TILE, PANEL)
+        at = (row, slice(None), slice(first, last))
+        return pltpu.make_async_remote_copy(
+            src_ref=g_own.at[at],
+            dst_ref=g_recv.at[at],
+            send_sem=gy_send.at[n],
+            recv_sem=gy_recv.at[n],
+            device_id=across,
+            device_id_type=MESH,
+        )
+
+    def gram(i):
+        pair = 2 * i
+        rows = TILE
+        left = jnp.concatenate([whi[pair], whi[pair + 1], wlo[pair], wlo[pair + 1]], axis=0)
+        count = 2 * (TILES - i)
+        right_hi = phi[pair : pair + count].reshape(count * 2 * per, depth)
+        right_lo = plo[pair : pair + count].reshape(count * 2 * per, depth)
+        both = bf16_nt(left, right_hi)
+        g_own[i, :, i * TILE :] = both[:rows] + both[rows:] + bf16_nt(left[:rows], right_lo)
+
+    @pl.loop(1, half_ring + 2)
+    def _(k):
+        @pl.when(k == 1)
+        def _():
+            convert_border(0)
+
+        @pl.when(k <= half_ring)
+        def _():
+            arrived(block_of(0, k), 0)
+            push(0, k, 0).start()
+
+        @pl.when(k < half_ring)
+        def _():
+            forward(0, k, 0).start()
+            arrived(block_of(1, k), 0)
+            push(1, k, 0).start()
+
+            @pl.when(k < half_ring - 1)
+            def _():
+                forward(1, k, 0).start()
+
+        @pl.when(k == 1)
+        def _():
+            convert_border(chunks // 2)
+
+        @pl.when(k == half_ring + 1)
+        def _():
+            for i in range(TILES):
+                gram(i)
+                if i == 0:
+                    g_piece(0).start()
+                g_piece(i + 1).start()
+
+        @pl.when(k > 1)
+        def _():
+            product_send(k - 1)
+
+        @pl.when(k <= half_ring)
+        def _():
+            arrived(block_of(1, k), 1)
+            push(1, k, 1).start()
+
+        @pl.when(k < half_ring)
+        def _():
+            forward(1, k, 1).start()
+            arrived(block_of(0, k), 1)
+            push(0, k, 1).start()
+
+            @pl.when(k < half_ring - 1)
+            def _():
+                forward(0, k, 1).start()
+
+        @pl.when(k > 1)
+        def _():
+            product(k - 1, scen, u_keep)
+
+        @pl.when(k <= half_ring)
+        def _():
+            for d in range(2):
+                @pl.when(k + d <= half_ring)
+                def _():
+                    which = block_of(d, k) // 2
+                    for h in range(2):
+                        arrived(2 * which + 1 - core, h)
+                    convert_both(which)
+
+        @pl.when(k == 1)
+        def _():
+            for h in range(2):
+                arrived(2 * chip + 1 - core, h)
+            convert(chip, core, lambda h: part_ref[h])
+            convert(chip, 1 - core, lambda h: gath[2 * chip + 1 - core, h])
+
+
+    t_ref[...] = jnp.zeros_like(t_ref)
+    g_piece(0).wait_recv()
+    t_ref[:TILE, :TILE] = g_own[0, :, :TILE] + g_recv[0, :, :TILE]
+
+    @pl.loop(0, TILES)
+    def _(j):
+        here = pl.ds(pl.multiple_of(j * TILE, TILE), TILE)
+        inv = inverse_factor(t_ref[here, here])
+        inv_ref[j] = inv
+
+        @pl.when(j == 0)
+        def _():
+            for i in range(TILES):
+                g_piece(i + 1).wait_recv()
+                lanes = slice(max(i, 1) * TILE, PANEL)
+                t_ref[i * TILE : (i + 1) * TILE, lanes] = g_own[i, :, lanes] + g_recv[i, :, lanes]
+
+        scaled = exact(inv, t_ref[here, :])
+        lane = lax.broadcasted_iota(jnp.int32, (TILE, PANEL), 1)
+        ahead = jnp.where(lane >= (j + 1) * TILE, scaled, 0.0).T
+        low_ref[:, here] = ahead
+        for i in range(1, TILES):
+
+            @pl.when(i > j)
+            def _():
+                part = slice(i * TILE, (i + 1) * TILE)
+                t_ref[part, :] -= exact(ahead[part], scaled)
+
+    for which in range(chips):
+        cross(which).wait_recv()
+    for j in range(TILES):
+        pair = slice(2 * j, 2 * j + 2)
+        v = (u_keep[pair] + u_recv[pair]).reshape(TILE, rows_owned)
+        if j > 0:
+            v -= exact(low_ref[j * TILE : (j + 1) * TILE, : j * TILE], x_ref[: j * TILE, :])
+        x = exact(inv_ref[j], v)
+        x_ref[j * TILE : (j + 1) * TILE, :] = x
+        out_ref[:, j * TILE : (j + 1) * TILE] = x.T
+
+    for h in range(2):
+        for d in range(3):
+            own(h, d).wait_send()
+    for k in range(1, half_ring + 1):
+        for d in range(2):
+            for h in range(2):
+                if k < half_ring - 1 or (k < half_ring and d == h):
+                    forward(d, k, h).wait_send()
+                if k < half_ring or d == h:
+                    push(d, k, h).wait_send()
+    for which in range(chips):
+        cross(which).wait_send()
+    for n in range(TILES + 1):
+        g_piece(n).wait_send()
+
+
+def ring_body(border, barrier, row_counts):
+    scen_here, capacity, own_cols = border.shape
+    n_col = lax.axis_size("col")
+    chips = n_col // 2
+    per = PANEL // n_col
+    depth = scen_here * capacity
+    rows_owned = own_cols // lax.axis_size("scen")
+    positions = lax.iota(jnp.int32, capacity)
+    weights = jnp.where(positions[None, :] < row_counts[:, None], 1.0 / barrier, jnp.float32(0.0))
+    part = jnp.transpose(border[:, :, :per], (0, 2, 1))
+    dma = pltpu.SemaphoreType.DMA
+    f32, bf16 = jnp.float32, jnp.bfloat16
+    solved = pl.pallas_call(
+        ring_kernel,
+        out_shape=jax.ShapeDtypeStruct((rows_owned, PANEL), f32),
+        in_specs=[
+            pl.BlockSpec(memory_space=pltpu.VMEM),
+            pl.BlockSpec(memory_space=pltpu.VMEM),
+            pl.BlockSpec(memory_space=pl.ANY),
+        ],
+        out_specs=pl.BlockSpec(memory_space=pltpu.VMEM),
+        scratch_shapes=[
+            pltpu.VMEM((n_col, scen_here, per, capacity), f32),
+            pltpu.VMEM((LAG, CHUNK, own_cols), f32),
+            pltpu.VMEM((depth, own_cols), bf16),
+            pltpu.VMEM((depth, own_cols), bf16),
+            *[pltpu.VMEM((chips, 2 * per, depth), bf16)] * 4,
+            *[pltpu.VMEM((chips, 2 * per, rows_owned), f32)] * 3,
+            *[pltpu.VMEM((TILES, TILE, PANEL), f32)] * 2,
+            pltpu.VMEM((PANEL, PANEL), f32),
+            pltpu.VMEM((TILES, TILE, TILE), f32),
+            pltpu.VMEM((PANEL, PANEL), f32),
+            pltpu.VMEM((PANEL, rows_owned), f32),
+            dma((LAG,)),
+            dma((2, chips // 2, 2)),
+            dma((chips + 1, 2)),
+            dma((n_col, 2)),
+            dma((chips,)),
+            dma((chips,)),
+            dma((TILES + 1,)),
+            dma((TILES + 1,)),
+        ],
+        compiler_params=pltpu.CompilerParams(
+            collective_id=0, has_side_effects=True, vmem_limit_bytes=60 * 2**20
+        ),
+        name="ring",
+    )(part, weights.reshape(scen_here, 1, capacity), border.reshape(depth, own_cols))
+    return solved.reshape(1, 1, rows_owned, PANEL)
+
+
 def solution(mesh):
+    n_scen, n_col = mesh.shape["scen"], mesh.shape["col"]
+    ring = n_scen == 2 and 4 * (PANEL // n_col) == TILE
     placed = (P("scen", None, "col"), P("scen", None), P("scen"))
     return jax.shard_map(
-        body, mesh=mesh, in_specs=placed, out_specs=P("col", "scen", None, None), check_vma=False
+        ring_body if ring else general_body,
+        mesh=mesh,
+        in_specs=placed,
+        out_specs=P("col", "scen", None, None),
+        check_vma=False,
     )

time: 143 us -> 87.9 us (0.61)
  waiting for transfers between devices: 64.1 us -> 0 us
  Pallas kernels: 28.8 us -> 81.3 us
  matrix products: 29.5 us -> 0 us
  between operations: 13.5 us -> 0.01 us
  starting transfers between devices: 2.09 us -> 0 us
  local copies, waits for them, and re-layouts: 3.91 us -> 5.57 us
    all_gather x1 -> x0, waiting for transfers between devices: 63.7 us -> none  [body(): panel = lax.all_gather(panel_part, 'col', axis=0, tiled=True)]
    pallas_call x1, Pallas kernels: 28.8 us -> 81.3 us  [ring_body(): pl.pallas_call(ring_kernel, out_shape=jax.ShapeDtypeStruct((rows_owned, P...]
    dot_general x3 -> x0, matrix products: 29.5 us -> none  [the longest x1 13.5 us: body(): jnp.einsum('pr,rc->pc', weighted, border.reshape(depth, own_cols), precis...]
    unnamed x13 -> x2, local copies, waits for them, and re-layouts: 0.11 us -> 3.46 us
    ppermute x2 -> x0, starting transfers between devices: 2.09 us -> none  [the longest x1 1.54 us: body(): upper_other = lax.ppermute(upper, 'scen', swap)]
  transfers between devices with their start and end apart: 3 -> 0, of which waited for: 2 -> 0; matrix products, arithmetic and copies ran while one was open for 11% -> 0% of each run, Pallas kernels for 20% -> 0%
where the time goes in v2:
time: 87.9 us; the launch traced here: 87.7 us
  Pallas kernels  81.3 us (92%)
  local copies, waits for them, and re-layouts  5.57 us (6%)
    pallas_call x1, Pallas kernels, ring_body(): pl.pallas_call(ring_kernel, out_shape=jax.ShapeDtypeStruct((rows_owned, P...  81.3 us
    unnamed x2, local copies, waits for them, and re-layouts  3.46 us

profile of v2, /device:TPU:0, one launch (start us, length us, event | category | flops | bytes accessed | tf_op | source)
XLA Modules:
  0.0 87.7 jit_solution(2607679958994784271)
XLA Ops:
  0.0 0.8 compare_select_fusion
  0.8 0.6 reshape.10.w_ref
  1.4 1.5 %slice.3 = f32[2,1536,32]{2,1,0:T(8,128)S(1)} slice(f32[2,1536,1024]{2,1,0:T(8,128)} %param.3), slice={[0:2], [0:1536], [0:32]} | slice | bytes 786432 | tf_op jit(solution)/shard_map/slice | solution.py:482
  2.9 1.2 %copy.5 = f32[2,1536,32]{1,2,0:T(8,128)} copy(f32[2,1536,32]{2,1,0:T(8,128)S(1)} %slice.3) | data formatting | bytes 786432
  4.1 81.3 %ring.1 = f32[512,512]{1,0:T(8,128)} custom-call(f32[2,32,1536]{2,1,0:T(8,128)} %bitcast.5, f32[2,1,1536]{2,1,0:T(1,128)} %reshape.10.w_ref, f32[3072,1024]{1,0:T(8,128)} %bitcast.3), custom_call_target="tpu_custom_call" | custom-call | tf_op jit(solution)/shard_map/ring/pallas_call | solution.py:485
  85.4 2.3 %copy.7 = f32[1,1,512,512]{3,2,1,0:T(8,128)} copy(f32[1,1,512,512]{3,2,1,0:T(8,128)} %bitcast.4) | data formatting | bytes 2097152

commit v3 on v2

--- a/solution.py
+++ b/solution.py
@@ -184,10 +184,10 @@
 
 
 def ring_kernel(
-    part_ref, w_ref, border_ref, out_ref,
-    gath, stage, bhi, blo, phi, plo, whi, wlo,
+    barrier_ref, counts_ref, border_ref, out_ref,
+    pan, part_ref, w_ref, gath, stage, bhi, blo, phi, plo, whi, wlo,
     u_keep, u_send, u_recv, g_own, g_recv, t_ref, inv_ref, low_ref, x_ref,
-    stage_sem, ring_send, core_send, recv_sem, uy_send, uy_recv, gy_send, gy_recv,
+    pan_sem, stage_sem, ring_send, core_send, recv_sem, uy_send, uy_recv, gy_send, gy_recv,
 ):
     chips = lax.axis_size("col") // 2
     half_ring = chips // 2
@@ -224,10 +224,18 @@
             stage_sem.at[n % LAG],
         )
 
+    def fetch_panel(h):
+        return pltpu.make_async_copy(
+            border_ref.at[pl.ds(h * depth_half, depth_half), pl.ds(0, TILE)],
+            pan.at[h],
+            pan_sem.at[h],
+        )
+
     chunks = depth // CHUNK
+    for h in range(2):
+        fetch_panel(h).start()
     for n in range(LAG):
         fetch(n).start()
-    pl.semaphore_wait(barrier, 4)
 
     def send(src, block, h, send_sem, peer):
         return pltpu.make_async_remote_copy(
@@ -258,8 +266,17 @@
         pltpu.make_async_copy(part_ref.at[h], gath.at[block, h], recv_sem.at[block, h]).wait()
 
     for h in range(2):
+        fetch_panel(h).wait()
+        for n in range(depth_half // TILE):
+            here = slice(n * TILE, (n + 1) * TILE)
+            part_ref[h, :, here] = pan[h, here, :].T[:per]
+        if h == 0:
+            pl.semaphore_wait(barrier, 4)
         for d in range(3):
             own(h, d).start()
+    place = lax.broadcasted_iota(jnp.int32, (1, depth_half), 1)
+    for h in range(2):
+        w_ref[h : h + 1, :] = jnp.where(place < counts_ref[h], 1.0 / barrier_ref[h : h + 1, :], 0.0)
 
     def convert_border(first):
         @pl.loop(first, first + chunks // 2)
@@ -279,20 +296,16 @@
             there = (which, pl.ds(cc * per, per), pl.ds(h * depth_half, depth_half))
             x = src(h)
             phi[there], plo[there] = split(x)
-            whi[there], wlo[there] = split(x * w_ref[h])
+            whi[there], wlo[there] = split(x * w_ref[h : h + 1, :])
 
     def convert_both(which):
         for cc in range(2):
             convert(which, cc, lambda h: gath[2 * which + cc, h])
 
-    def unit(k):
-        first = chip_at(pos - k)
-        return first, chip_at(pos + k * (1 - k // half_ring))
-
-    def product(k, which, dst):
-        a, b = unit(k)
-        left = jnp.concatenate([whi[a], whi[b], wlo[a], wlo[b]], axis=0)
-        rows = 2 * whi.shape[1]
+    def product(unit, which, dst):
+        left = jnp.concatenate([ref[a] for ref in (whi, wlo) for a in unit], axis=0)
+        rows = left.shape[0] // 2
+        each = whi.shape[1]
 
         @pl.loop(0, rows_owned // CHUNK)
         def _(n):
@@ -300,8 +313,8 @@
             to = pl.ds(pl.multiple_of(n * CHUNK, CHUNK), CHUNK)
             both = bf16_nn(left, bhi[:, col])
             res = both[:rows] + both[rows:] + bf16_nn(left[:rows], blo[:, col])
-            dst[a, :, to] = res[: rows // 2]
-            dst[b, :, to] = res[rows // 2 :]
+            for n, a in enumerate(unit):
+                dst[a, :, to] = res[n * each : (n + 1) * each]
 
     def cross(which):
         return pltpu.make_async_remote_copy(
@@ -313,9 +326,9 @@
             device_id_type=MESH,
         )
 
-    def product_send(k):
-        product(k, 1 - scen, u_send)
-        for which in unit(k):
+    def product_send(unit):
+        product(unit, 1 - scen, u_send)
+        for which in unit:
             cross(which).start()
 
     def g_piece(n):
@@ -339,120 +352,115 @@
         right_hi = phi[pair : pair + count].reshape(count * 2 * per, depth)
         right_lo = plo[pair : pair + count].reshape(count * 2 * per, depth)
         both = bf16_nt(left, right_hi)
-        g_own[i, :, i * TILE :] = both[:rows] + both[rows:] + bf16_nt(left[:rows], right_lo)
-
-    @pl.loop(1, half_ring + 2)
+        res = both[:rows] + both[rows:] + bf16_nt(left[:rows], right_lo)
+        g_own[i, :, i * TILE :] = res
+        t_ref[i * TILE : (i + 1) * TILE, i * TILE :] = res
+
+    def receive(d, k, h, first):
+        block = block_of(d, k)
+        arrived(block, h)
+        push(d, k, h).start()
+
+        @pl.when(k < half_ring - 1 + first)
+        def _():
+            forward(d, k, h).start()
+
+    @pl.loop(1, half_ring)
     def _(k):
         @pl.when(k == 1)
         def _():
             convert_border(0)
 
-        @pl.when(k <= half_ring)
-        def _():
-            arrived(block_of(0, k), 0)
-            push(0, k, 0).start()
-
-        @pl.when(k < half_ring)
-        def _():
-            forward(0, k, 0).start()
-            arrived(block_of(1, k), 0)
-            push(1, k, 0).start()
-
-            @pl.when(k < half_ring - 1)
-            def _():
-                forward(1, k, 0).start()
+        receive(0, k, 0, 1)
+        receive(1, k, 0, 0)
 
         @pl.when(k == 1)
         def _():
             convert_border(chunks // 2)
-
-        @pl.when(k == half_ring + 1)
-        def _():
-            for i in range(TILES):
-                gram(i)
-                if i == 0:
-                    g_piece(0).start()
-                g_piece(i + 1).start()
-
-        @pl.when(k > 1)
-        def _():
-            product_send(k - 1)
-
-        @pl.when(k <= half_ring)
-        def _():
-            arrived(block_of(1, k), 1)
-            push(1, k, 1).start()
-
-        @pl.when(k < half_ring)
-        def _():
-            forward(1, k, 1).start()
-            arrived(block_of(0, k), 1)
-            push(0, k, 1).start()
-
-            @pl.when(k < half_ring - 1)
-            def _():
-                forward(0, k, 1).start()
-
-        @pl.when(k > 1)
-        def _():
-            product(k - 1, scen, u_keep)
-
-        @pl.when(k <= half_ring)
-        def _():
-            for d in range(2):
-                @pl.when(k + d <= half_ring)
-                def _():
-                    which = block_of(d, k) // 2
-                    for h in range(2):
-                        arrived(2 * which + 1 - core, h)
-                    convert_both(which)
-
-        @pl.when(k == 1)
-        def _():
             for h in range(2):
                 arrived(2 * chip + 1 - core, h)
             convert(chip, core, lambda h: part_ref[h])
             convert(chip, 1 - core, lambda h: gath[2 * chip + 1 - core, h])
-
-
-    t_ref[...] = jnp.zeros_like(t_ref)
+            product_send([chip])
+
+        before = [chip_at(pos - k + 1), chip_at(pos + k - 1)]
+
+        @pl.when(k > 1)
+        def _():
+            product_send(before)
+
+        receive(1, k, 1, 1)
+        receive(0, k, 1, 0)
+
+        @pl.when(k == 1)
+        def _():
+            product([chip], scen, u_keep)
+
+        @pl.when(k > 1)
+        def _():
+            product(before, scen, u_keep)
+
+        for d in range(2):
+            which = block_of(d, k) // 2
+            for h in range(2):
+                arrived(2 * which + 1 - core, h)
+            convert_both(which)
+
+    last = [chip_at(pos - half_ring + 1), chip_at(pos + half_ring - 1)]
+    far = chip_at(pos + half_ring)
+    product_send(last)
+    for h in range(2):
+        arrived(block_of(h, half_ring), h)
+        push(h, half_ring, h).start()
+    product(last, scen, u_keep)
+    for h in range(2):
+        arrived(2 * far + 1 - core, h)
+    convert_both(far)
+    for i in range(TILES):
+        gram(i)
+        if i == 0:
+            g_piece(0).start()
+        g_piece(i + 1).start()
+    product_send([far])
+    product([far], scen, u_keep)
+
+    def tiles(i):
+        return slice(i * TILE, (i + 1) * TILE)
+
     g_piece(0).wait_recv()
-    t_ref[:TILE, :TILE] = g_own[0, :, :TILE] + g_recv[0, :, :TILE]
-
-    @pl.loop(0, TILES)
-    def _(j):
-        here = pl.ds(pl.multiple_of(j * TILE, TILE), TILE)
-        inv = inverse_factor(t_ref[here, here])
+    t_ref[:TILE, :TILE] += g_recv[0, :, :TILE]
+    inv = inverse_factor(t_ref[:TILE, :TILE])
+    g_piece(1).wait_recv()
+    t_ref[:TILE, TILE:] += g_recv[0, :, TILE:]
+    for j in range(TILES):
         inv_ref[j] = inv
-
-        @pl.when(j == 0)
-        def _():
+        if j == TILES - 1:
+            break
+        scaled = exact(inv, t_ref[tiles(j), (j + 1) * TILE :])
+        ahead = scaled.T
+        low_ref[(j + 1) * TILE :, tiles(j)] = ahead
+        g_piece(j + 2).wait_recv()
+        t_ref[tiles(j + 1), (j + 1) * TILE :] += g_recv[j + 1, :, (j + 1) * TILE :]
+        if j == TILES - 2:
+            for which in range(chips):
+                cross(which).wait_recv()
+        pivot = t_ref[tiles(j + 1), tiles(j + 1)] - exact(ahead[:TILE], scaled[:, :TILE])
+        inv = inverse_factor(pivot)
+        for i in range(j + 1, TILES):
+            first = max(i, j + 2)
+            if first < TILES:
+                t_ref[tiles(i), first * TILE :] -= exact(
+                    ahead[tiles(i - j - 1)], scaled[:, (first - j - 1) * TILE :]
+                )
+        if j == TILES - 2:
             for i in range(TILES):
-                g_piece(i + 1).wait_recv()
-                lanes = slice(max(i, 1) * TILE, PANEL)
-                t_ref[i * TILE : (i + 1) * TILE, lanes] = g_own[i, :, lanes] + g_recv[i, :, lanes]
-
-        scaled = exact(inv, t_ref[here, :])
-        lane = lax.broadcasted_iota(jnp.int32, (TILE, PANEL), 1)
-        ahead = jnp.where(lane >= (j + 1) * TILE, scaled, 0.0).T
-        low_ref[:, here] = ahead
-        for i in range(1, TILES):
-
-            @pl.when(i > j)
-            def _():
-                part = slice(i * TILE, (i + 1) * TILE)
-                t_ref[part, :] -= exact(ahead[part], scaled)
-
-    for which in range(chips):
-        cross(which).wait_recv()
-    for j in range(TILES):
-        pair = slice(2 * j, 2 * j + 2)
-        v = (u_keep[pair] + u_recv[pair]).reshape(TILE, rows_owned)
-        if j > 0:
-            v -= exact(low_ref[j * TILE : (j + 1) * TILE, : j * TILE], x_ref[: j * TILE, :])
-        x = exact(inv_ref[j], v)
-        x_ref[j * TILE : (j + 1) * TILE, :] = x
-        out_ref[:, j * TILE : (j + 1) * TILE] = x.T
+                pair = slice(2 * i, 2 * i + 2)
+                x_ref[tiles(i), :] = (u_keep[pair] + u_recv[pair]).reshape(TILE, rows_owned)
+            for i in range(TILES - 1):
+                x = exact(inv_ref[i], x_ref[tiles(i), :])
+                out_ref[:, tiles(i)] = x.T
+                x_ref[(i + 1) * TILE :, :] -= exact(low_ref[(i + 1) * TILE :, tiles(i)], x)
+    out_ref[:, tiles(TILES - 1)] = exact(inv, x_ref[tiles(TILES - 1), :]).T
 
     for h in range(2):
         for d in range(3):
@@ -477,9 +485,6 @@
     per = PANEL // n_col
     depth = scen_here * capacity
     rows_owned = own_cols // lax.axis_size("scen")
-    positions = lax.iota(jnp.int32, capacity)
-    weights = jnp.where(positions[None, :] < row_counts[:, None], 1.0 / barrier, jnp.float32(0.0))
-    part = jnp.transpose(border[:, :, :per], (0, 2, 1))
     dma = pltpu.SemaphoreType.DMA
     f32, bf16 = jnp.float32, jnp.bfloat16
     solved = pl.pallas_call(
@@ -487,11 +492,14 @@
         out_shape=jax.ShapeDtypeStruct((rows_owned, PANEL), f32),
         in_specs=[
             pl.BlockSpec(memory_space=pltpu.VMEM),
-            pl.BlockSpec(memory_space=pltpu.VMEM),
+            pl.BlockSpec(memory_space=pltpu.SMEM),
             pl.BlockSpec(memory_space=pl.ANY),
         ],
         out_specs=pl.BlockSpec(memory_space=pltpu.VMEM),
         scratch_shapes=[
+            pltpu.VMEM((scen_here, capacity, TILE), f32),
+            pltpu.VMEM((scen_here, per, capacity), f32),
+            pltpu.VMEM((scen_here, capacity), f32),
             pltpu.VMEM((n_col, scen_here, per, capacity), f32),
             pltpu.VMEM((LAG, CHUNK, own_cols), f32),
             pltpu.VMEM((depth, own_cols), bf16),
@@ -503,6 +511,7 @@
             pltpu.VMEM((TILES, TILE, TILE), f32),
             pltpu.VMEM((PANEL, PANEL), f32),
             pltpu.VMEM((PANEL, rows_owned), f32),
+            dma((scen_here,)),
             dma((LAG,)),
             dma((2, chips // 2, 2)),
             dma((chips + 1, 2)),
@@ -516,7 +525,7 @@
             collective_id=0, has_side_effects=True, vmem_limit_bytes=60 * 2**20
         ),
         name="ring",
-    )(part, weights.reshape(scen_here, 1, capacity), border.reshape(depth, own_cols))
+    )(barrier, row_counts, border.reshape(depth, own_cols))
     return solved.reshape(1, 1, rows_owned, PANEL)
 
 

time: 87.9 us -> 75.2 us (0.86)
  Pallas kernels: 81.3 us -> 72.7 us
  local copies, waits for them, and re-layouts: 5.57 us -> 2.26 us
    pallas_call x1, Pallas kernels: 81.3 us -> 72.7 us  [ring_body(): pl.pallas_call(ring_kernel, out_shape=jax.ShapeDtypeStruct((rows_owned, P...]
    slice x1 -> x0, local copies, waits for them, and re-layouts: 1.51 us -> none  [ring_body(): part = jnp.transpose(border[:, :, :per], (0, 2, 1))]
    unnamed x2 -> x1, local copies, waits for them, and re-layouts: 3.46 us -> 2.26 us
where the time goes in v3:
time: 75.2 us; the launch traced here: 75 us
  Pallas kernels  72.7 us (97%)
  local copies, waits for them, and re-layouts  2.26 us (3%)
    pallas_call x1, Pallas kernels, ring_body(): pl.pallas_call(ring_kernel, out_shape=jax.ShapeDtypeStruct((rows_owned, P...  72.7 us
    unnamed x1, local copies, waits for them, and re-layouts  2.26 us

profile of v3, /device:TPU:0, one launch (start us, length us, event | category | flops | bytes accessed | tf_op | source)
XLA Modules:
  0.0 75.0 jit_solution(8082884691809699201)
XLA Ops:
  0.0 72.7 %ring.1 = f32[512,512]{1,0:T(8,128)} custom-call(f32[2,1536]{1,0:T(2,128)} %barrier_ref.1, s32[2]{0:T(128)} %counts_ref.1, f32[3072,1024]{1,0:T(8,128)} %bitcast.2), custom_call_target="tpu_custom_call" | custom-call | tf_op jit(solution)/shard_map/ring/pallas_call | solution.py:490
  72.7 2.3 %copy.5 = f32[1,1,512,512]{3,2,1,0:T(8,128)} copy(f32[1,1,512,512]{3,2,1,0:T(8,128)} %bitcast.3) | data formatting | bytes 2097152

commit v4 on v3

--- a/solution.py
+++ b/solution.py
@@ -18,58 +18,66 @@
         xs=[xs[i]+xs[i+1] if i+1<len(xs) else xs[i] for i in range(0,len(xs),2)]
     return xs[0]
 
+def lane_of(x, c):
+    return jnp.take_along_axis(x, jnp.full((SUB, TILE), c, jnp.int32), axis=1)
+
+
+def row_of(x, i):
+    return jnp.take_along_axis(x, jnp.full((SUB, TILE), i, jnp.int32), axis=0)
+
+
 def inverse_factor(a):
-    n=TILE//SUB
-    lane = lax.broadcasted_iota(jnp.int32,(SUB,TILE),1)
-    sub = lax.broadcasted_iota(jnp.int32,(SUB,TILE),0)
-    rows=[a[SUB*t:SUB*(t+1)] for t in range(n)]
-    out=[]
-    B=lambda x: jnp.broadcast_to(x,(SUB,TILE))
+    n = TILE // SUB
+    lane = lax.broadcasted_iota(jnp.int32, (SUB, TILE), 1)
+    sub = lax.broadcasted_iota(jnp.int32, (SUB, TILE), 0)
+    rows = [a[SUB * t : SUB * (t + 1)] for t in range(n)]
+    out = []
+    each = range(SUB)
     for g in range(n):
-        c0=g*SUB
-        d=rows[g]
-        inb=(lane>=c0)&(lane<c0+SUB)
-        cols=[B(d[:,c0+j:c0+j+1]) for j in range(SUB)]
-        A={}
-        for j in range(SUB):
-            for i in range(j,SUB):
-                A[i,j]=B(cols[j][i:i+1])
-        r=[None]*SUB; dd=[None]*SUB; M={}
-        for k in range(SUB):
-            dd[k]=A[k,k]
-            r[k]=1.0/dd[k]
-            for i in range(k+1,SUB):
-                M[i,k]=A[i,k]*r[k]
-            for j in range(k+1,SUB):
-                for i in range(j,SUB):
-                    A[i,j]=A[i,j]-M[i,k]*A[j,k] if i!=j else A[i,j]-M[i,k]*A[i,k]
-        N={}
-        for j in range(SUB):
-            for i in range(j+1,SUB):
-                s=M[i,j]
-                for k in range(j+1,i):
-                    s=s+M[i,k]*N[k,j]
-                N[i,j]=-s
-        dp=jnp.where(inb, jnp.where(lane-c0==sub,1.0,0.0), d)
-        drow=[B(dp[j:j+1]) for j in range(SUB)]
-        ncol=[]
-        for j in range(SUB-1):
-            m=jnp.zeros((SUB,TILE),jnp.float32)
-            for i in range(j+1,SUB):
-                m=jnp.where(sub==i,N[i,j],m)
-            ncol.append(m)
-        u=tree([dp]+[ncol[j]*drow[j] for j in range(SUB-1)])
-        dvec=dd[0]
-        for i in range(1,SUB):
-            dvec=jnp.where(sub==i,dd[i],dvec)
-        out.append(jnp.where(lane<c0+SUB,u*lax.rsqrt(dvec),0.0))
-        if g==n-1: break
-        ub=[B(u[i:i+1])*r[i] for i in range(SUB)]
-        Z=[tree([ub[j]]+[N[i,j]*ub[i] for i in range(j+1,SUB)]) for j in range(SUB)]
-        for t in range(g+1,n):
-            cb=[B(rows[t][:,c0+j:c0+j+1]) for j in range(SUB)]
-            rows[t]=jnp.where(inb,0.0,rows[t])-tree([cb[j]*Z[j] for j in range(SUB)])
-    return jnp.concatenate(out,axis=0)
+        c0 = g * SUB
+        d = rows[g]
+        inside = (lane >= c0) & (lane < c0 + SUB)
+        cols = [lane_of(d, c0 + j) for j in each]
+        s = {(i, j): row_of(cols[j], i) for j in each for i in range(j, SUB)}
+        mixed = jnp.where(inside, jnp.where(lane - c0 == sub, 1.0, 0.0), d)
+        u = [row_of(mixed, i) for i in each]
+        more = g + 1 < n
+        if more:
+            below = [lane_of(rows[g + 1], c0 + j) for j in each]
+            ahead = jnp.where(inside, 0.0, rows[g + 1])
+        m, ur = {}, []
+        for k in each:
+            r = 1.0 / s[k, k]
+            for i in range(k + 1, SUB):
+                m[i, k] = s[i, k] * r
+            for j in range(k + 1, SUB):
+                for i in range(j, SUB):
+                    s[i, j] = s[i, j] - m[i, k] * s[j, k]
+            ur.append(u[k] * r)
+            for i in range(k + 1, SUB):
+                u[i] = u[i] - m[i, k] * u[k]
+            if more:
+                for i in range(k + 1, SUB):
+                    below[i] = below[i] - m[i, k] * below[k]
+                ahead = ahead - below[k] * ur[k]
+        whole, pivot = u[0], s[0, 0]
+        for i in range(1, SUB):
+            whole = jnp.where(sub == i, u[i], whole)
+            pivot = jnp.where(sub == i, s[i, i], pivot)
+        out.append(jnp.where(lane < c0 + SUB, whole * lax.rsqrt(pivot), 0.0))
+        if not more:
+            break
+        rows[g + 1] = ahead
+        z = [None] * SUB
+        for j in reversed(each):
+            z[j] = ur[j]
+            for i in range(j + 1, SUB):
+                z[j] = z[j] - m[i, j] * z[i]
+        for t in range(g + 2, n):
+            terms = [lane_of(rows[t], c0 + j) * z[j] for j in each]
+            rows[t] = jnp.where(inside, 0.0, rows[t]) - tree(terms)
+    return jnp.concatenate(out, axis=0)
+
 
 def factor_kernel(a_ref, b_ref, inv_ref, t_ref):
     t_ref[...] = jnp.zeros_like(t_ref)
@@ -187,7 +195,7 @@
     barrier_ref, counts_ref, border_ref, out_ref,
     pan, part_ref, w_ref, gath, stage, bhi, blo, phi, plo, whi, wlo,
     u_keep, u_send, u_recv, g_own, g_recv, t_ref, inv_ref, low_ref, x_ref,
-    pan_sem, stage_sem, ring_send, core_send, recv_sem, uy_send, uy_recv, gy_send, gy_recv,
+    pan_sem, stage_sem, ring_send, core_send, recv_sem, uy_send, uy_recv, gy_send, gy_recv, g_push_sem,
 ):
     chips = lax.axis_size("col") // 2
     half_ring = chips // 2
@@ -302,19 +310,24 @@
         for cc in range(2):
             convert(which, cc, lambda h: gath[2 * which + cc, h])
 
-    def product(unit, which, dst):
+    def product(unit, which, dst, unroll=False):
         left = jnp.concatenate([ref[a] for ref in (whi, wlo) for a in unit], axis=0)
         rows = left.shape[0] // 2
         each = whi.shape[1]
 
-        @pl.loop(0, rows_owned // CHUNK)
-        def _(n):
+        def columns(n):
             col = pl.ds(pl.multiple_of(which * rows_owned + n * CHUNK, CHUNK), CHUNK)
             to = pl.ds(pl.multiple_of(n * CHUNK, CHUNK), CHUNK)
             both = bf16_nn(left, bhi[:, col])
             res = both[:rows] + both[rows:] + bf16_nn(left[:rows], blo[:, col])
-            for n, a in enumerate(unit):
-                dst[a, :, to] = res[n * each : (n + 1) * each]
+            for i, a in enumerate(unit):
+                dst[a, :, to] = res[i * each : (i + 1) * each]
+
+        if unroll:
+            for n in range(rows_owned // CHUNK):
+                columns(n)
+        else:
+            pl.loop(0, rows_owned // CHUNK)(columns)
 
     def cross(which):
         return pltpu.make_async_remote_copy(
@@ -326,15 +339,47 @@
             device_id_type=MESH,
         )
 
-    def product_send(unit):
-        product(unit, 1 - scen, u_send)
+    def product_send(unit, unroll=False):
+        product(unit, 1 - scen, u_send, unroll)
         for which in unit:
             cross(which).start()
 
-    def g_piece(n):
+    def g_at(n):
         row = max(n - 1, 0)
         first, last = (0, TILE) if n == 0 else (max(row, 1) * TILE, PANEL)
-        at = (row, slice(None), slice(first, last))
+        return row, slice(None), slice(first, last)
+
+    def g_owner(n):
+        return (n // 2) % 2
+
+    def g_start(n):
+        @pl.when(core == g_owner(n))
+        def _():
+            g_piece(n).start()
+
+    def g_push(n):
+        return pltpu.make_async_remote_copy(
+            src_ref=g_recv.at[g_at(n)],
+            dst_ref=g_recv.at[g_at(n)],
+            send_sem=g_push_sem.at[n],
+            recv_sem=gy_recv.at[n],
+            device_id=mate,
+            device_id_type=MESH,
+        )
+
+    def g_relay(n):
+        @pl.when(core == g_owner(n))
+        def _():
+            g_piece(n).wait_recv()
+            g_push(n).start()
+
+    def g_wait(n):
+        @pl.when(core != g_owner(n))
+        def _():
+            g_piece(n).wait_recv()
+
+    def g_piece(n):
+        at = g_at(n)
         return pltpu.make_async_remote_copy(
             src_ref=g_own.at[at],
             dst_ref=g_recv.at[at],
@@ -416,13 +461,12 @@
     for h in range(2):
         arrived(2 * far + 1 - core, h)
     convert_both(far)
-    for i in range(TILES):
+    gram(0)
+    g_piece(0).start()
+    g_start(1)
+    for i in range(1, TILES):
         gram(i)
-        if i == 0:
-            g_piece(0).start()
-        g_piece(i + 1).start()
-    product_send([far])
-    product([far], scen, u_keep)
+        g_start(i + 1)
 
     def tiles(i):
         return slice(i * TILE, (i + 1) * TILE)
@@ -430,16 +474,24 @@
     g_piece(0).wait_recv()
     t_ref[:TILE, :TILE] += g_recv[0, :, :TILE]
     inv = inverse_factor(t_ref[:TILE, :TILE])
-    g_piece(1).wait_recv()
+    product([far], 1 - scen, u_send, True)
+    product([far], scen, u_keep, True)
+    cross(far).start()
+    g_relay(1)
+    g_relay(2)
+    g_wait(1)
     t_ref[:TILE, TILE:] += g_recv[0, :, TILE:]
     for j in range(TILES):
         inv_ref[j] = inv
         if j == TILES - 1:
             break
+        if j == 1:
+            g_relay(3)
+            g_relay(4)
         scaled = exact(inv, t_ref[tiles(j), (j + 1) * TILE :])
         ahead = scaled.T
         low_ref[(j + 1) * TILE :, tiles(j)] = ahead
-        g_piece(j + 2).wait_recv()
+        g_wait(j + 2)
         t_ref[tiles(j + 1), (j + 1) * TILE :] += g_recv[j + 1, :, (j + 1) * TILE :]
         if j == TILES - 2:
             for which in range(chips):
@@ -474,8 +526,13 @@
                     push(d, k, h).wait_send()
     for which in range(chips):
         cross(which).wait_send()
-    for n in range(TILES + 1):
-        g_piece(n).wait_send()
+    g_piece(0).wait_send()
+    for n in range(1, TILES + 1):
+
+        @pl.when(core == g_owner(n))
+        def _():
+            g_piece(n).wait_send()
+            g_push(n).wait_send()
 
 
 def ring_body(border, barrier, row_counts):
@@ -520,6 +577,7 @@
             dma((chips,)),
             dma((TILES + 1,)),
             dma((TILES + 1,)),
+            dma((TILES + 1,)),
         ],
         compiler_params=pltpu.CompilerParams(
             collective_id=0, has_side_effects=True, vmem_limit_bytes=60 * 2**20

time: 75.2 us -> 69.2 us (0.920)
  Pallas kernels: 72.7 us -> 66.7 us
    pallas_call x1, Pallas kernels: 72.7 us -> 66.7 us  [ring_body(): pl.pallas_call(ring_kernel, out_shape=jax.ShapeDtypeStruct((rows_owned, P...]
where the time goes in v4:
time: 69.2 us; the launch traced here: 68.9 us
  Pallas kernels  66.7 us (96%)
  local copies, waits for them, and re-layouts  2.26 us (3%)
    pallas_call x1, Pallas kernels, ring_body(): pl.pallas_call(ring_kernel, out_shape=jax.ShapeDtypeStruct((rows_owned, P...  66.7 us
    unnamed x1, local copies, waits for them, and re-layouts  2.26 us

profile of v4, /device:TPU:0, one launch (start us, length us, event | category | flops | bytes accessed | tf_op | source)
XLA Modules:
  0.0 68.9 jit_solution(12215104541731276810)
XLA Ops:
  0.0 66.7 %ring.1 = f32[512,512]{1,0:T(8,128)} custom-call(f32[2,1536]{1,0:T(2,128)} %barrier_ref.1, s32[2]{0:T(128)} %counts_ref.1, f32[3072,1024]{1,0:T(8,128)} %bitcast.2), custom_call_target="tpu_custom_call" | custom-call | tf_op jit(solution)/shard_map/ring/pallas_call | solution.py:547
  66.7 2.3 %copy.5 = f32[1,1,512,512]{3,2,1,0:T(8,128)} copy(f32[1,1,512,512]{3,2,1,0:T(8,128)} %bitcast.3) | data formatting | bytes 2097152

commit v5 on v4

--- a/solution.py
+++ b/solution.py
@@ -195,7 +195,7 @@
     barrier_ref, counts_ref, border_ref, out_ref,
     pan, part_ref, w_ref, gath, stage, bhi, blo, phi, plo, whi, wlo,
     u_keep, u_send, u_recv, g_own, g_recv, t_ref, inv_ref, low_ref, x_ref,
-    pan_sem, stage_sem, ring_send, core_send, recv_sem, uy_send, uy_recv, gy_send, gy_recv, g_push_sem,
+    pan_sem, stage_sem, ring_send, core_send, recv_sem, uy_send, uy_recv, gy_send, gy_recv, g_push_sem, g_share_send, g_share_recv,
 ):
     chips = lax.axis_size("col") // 2
     half_ring = chips // 2
@@ -242,8 +242,6 @@
     chunks = depth // CHUNK
     for h in range(2):
         fetch_panel(h).start()
-    for n in range(LAG):
-        fetch(n).start()
 
     def send(src, block, h, send_sem, peer):
         return pltpu.make_async_remote_copy(
@@ -282,6 +280,8 @@
             pl.semaphore_wait(barrier, 4)
         for d in range(3):
             own(h, d).start()
+    for n in range(LAG):
+        fetch(n).start()
     place = lax.broadcasted_iota(jnp.int32, (1, depth_half), 1)
     for h in range(2):
         w_ref[h : h + 1, :] = jnp.where(place < counts_ref[h], 1.0 / barrier_ref[h : h + 1, :], 0.0)
@@ -352,10 +352,15 @@
     def g_owner(n):
         return (n // 2) % 2
 
-    def g_start(n):
-        @pl.when(core == g_owner(n))
-        def _():
-            g_piece(n).start()
+    def g_share(n):
+        return pltpu.make_async_remote_copy(
+            src_ref=g_own.at[g_at(n)],
+            dst_ref=g_own.at[g_at(n)],
+            send_sem=g_share_send.at[n],
+            recv_sem=g_share_recv.at[n],
+            device_id=mate,
+            device_id_type=MESH,
+        )
 
     def g_push(n):
         return pltpu.make_async_remote_copy(
@@ -377,6 +382,7 @@
         @pl.when(core != g_owner(n))
         def _():
             g_piece(n).wait_recv()
+            g_share(n).wait_recv()
 
     def g_piece(n):
         at = g_at(n)
@@ -389,17 +395,19 @@
             device_id_type=MESH,
         )
 
-    def gram(i):
-        pair = 2 * i
-        rows = TILE
-        left = jnp.concatenate([whi[pair], whi[pair + 1], wlo[pair], wlo[pair + 1]], axis=0)
-        count = 2 * (TILES - i)
-        right_hi = phi[pair : pair + count].reshape(count * 2 * per, depth)
-        right_lo = plo[pair : pair + count].reshape(count * 2 * per, depth)
+    def gram(n):
+        row, _, lanes = g_at(n)
+        left = jnp.concatenate(
+            [ref[2 * row + a] for ref in (whi, wlo) for a in range(2)], axis=0
+        )
+        pairs = slice(2 * lanes.start // TILE, 2 * lanes.stop // TILE)
+        right_hi = phi[pairs].reshape(lanes.stop - lanes.start, depth)
+        right_lo = plo[pairs].reshape(lanes.stop - lanes.start, depth)
         both = bf16_nt(left, right_hi)
-        res = both[:rows] + both[rows:] + bf16_nt(left[:rows], right_lo)
-        g_own[i, :, i * TILE :] = res
-        t_ref[i * TILE : (i + 1) * TILE, i * TILE :] = res
+        g_own[g_at(n)] = both[:TILE] + both[TILE:] + bf16_nt(left[:TILE], right_lo)
+        g_piece(n).start()
+        if n > 0:
+            g_share(n).start()
 
     def receive(d, k, h, first):
         block = block_of(d, k)
@@ -462,37 +470,40 @@
         arrived(2 * far + 1 - core, h)
     convert_both(far)
     gram(0)
-    g_piece(0).start()
-    g_start(1)
-    for i in range(1, TILES):
-        gram(i)
-        g_start(i + 1)
+    for owner in range(2):
+
+        @pl.when(core == owner)
+        def _():
+            for n in range(1, TILES + 1):
+                if g_owner(n) == owner:
+                    gram(n)
+
+    t_ref[...] = jnp.zeros_like(t_ref)
 
     def tiles(i):
         return slice(i * TILE, (i + 1) * TILE)
 
     g_piece(0).wait_recv()
-    t_ref[:TILE, :TILE] += g_recv[0, :, :TILE]
-    inv = inverse_factor(t_ref[:TILE, :TILE])
+    inv = inverse_factor(g_own[0, :, :TILE] + g_recv[0, :, :TILE])
     product([far], 1 - scen, u_send, True)
-    product([far], scen, u_keep, True)
     cross(far).start()
     g_relay(1)
     g_relay(2)
+    product([far], scen, u_keep, True)
+    g_relay(3)
+    g_relay(4)
     g_wait(1)
-    t_ref[:TILE, TILE:] += g_recv[0, :, TILE:]
+    t_ref[:TILE, TILE:] += g_own[0, :, TILE:] + g_recv[0, :, TILE:]
     for j in range(TILES):
         inv_ref[j] = inv
         if j == TILES - 1:
             break
-        if j == 1:
-            g_relay(3)
-            g_relay(4)
         scaled = exact(inv, t_ref[tiles(j), (j + 1) * TILE :])
         ahead = scaled.T
         low_ref[(j + 1) * TILE :, tiles(j)] = ahead
         g_wait(j + 2)
-        t_ref[tiles(j + 1), (j + 1) * TILE :] += g_recv[j + 1, :, (j + 1) * TILE :]
+        right = slice((j + 1) * TILE, PANEL)
+        t_ref[tiles(j + 1), right] += g_own[j + 1, :, right] + g_recv[j + 1, :, right]
         if j == TILES - 2:
             for which in range(chips):
                 cross(which).wait_recv()
@@ -533,6 +544,7 @@
         def _():
             g_piece(n).wait_send()
             g_push(n).wait_send()
+            g_share(n).wait_send()
 
 
 def ring_body(border, barrier, row_counts):
@@ -575,12 +587,10 @@
             dma((n_col, 2)),
             dma((chips,)),
             dma((chips,)),
-            dma((TILES + 1,)),
-            dma((TILES + 1,)),
-            dma((TILES + 1,)),
+            *[dma((TILES + 1,))] * 5,
         ],
         compiler_params=pltpu.CompilerParams(
-            collective_id=0, has_side_effects=True, vmem_limit_bytes=60 * 2**20
+            collective_id=0, has_side_effects=True, vmem_limit_bytes=50 * 2**20
         ),
         name="ring",
     )(barrier, row_counts, border.reshape(depth, own_cols))

time: 69.2 us -> 67.6 us (0.977)
  Pallas kernels: 66.7 us -> 65.1 us
    pallas_call x1, Pallas kernels: 66.7 us -> 65.1 us  [ring_body(): pl.pallas_call(ring_kernel, out_shape=jax.ShapeDtypeStruct((rows_owned, P...]
    unnamed x1 -> x5, local copies, waits for them, and re-layouts: 2.26 us -> 2.33 us
where the time goes in v5:
time: 67.6 us; the launch traced here: 67.4 us
  Pallas kernels  65.1 us (96%)
  local copies, waits for them, and re-layouts  2.33 us (3%)
    pallas_call x1, Pallas kernels, ring_body(): pl.pallas_call(ring_kernel, out_shape=jax.ShapeDtypeStruct((rows_owned, P...  65.1 us
    unnamed x5, local copies, waits for them, and re-layouts  2.33 us

profile of v5, /device:TPU:0, one launch (start us, length us, event | category | flops | bytes accessed | tf_op | source)
XLA Modules:
  0.0 67.4 jit_solution(5659096109546957500)
XLA Ops:
  0.0 0.0 copy-start
  0.0 0.7 %copy-done = f32[2,1536]{1,0:T(2,128)S(1)} copy-done((f32[2,1536]{1,0:T(2,128)S(1)}, f32[2,1536]{1,0:T(2,128)}, u32[]{:S(2)}) %copy-start) | copy-done | bytes 12312
  0.7 0.0 copy-start.1
  0.7 0.7 copy-done.1
  1.4 65.1 %ring.1 = f32[512,512]{1,0:T(8,128)S(1)} custom-call(f32[2,1536]{1,0:T(2,128)S(1)} %copy-done, s32[2]{0:T(128)S(1)} %copy-done.1, f32[3072,1024]{1,0:T(8,128)} %bitcast.3), custom_call_target="tpu_custom_call" | custom-call | tf_op jit(solution)/shard_map/ring/pallas_call | solution.py:559
  66.4 1.0 %copy.5 = f32[1,1,512,512]{3,2,1,0:T(8,128)} copy(f32[1,1,512,512]{3,2,1,0:T(8,128)S(1)} %bitcast.2) | data formatting | bytes 2097152
Async XLA Ops:
  0.0 0.7 %copy-start = (f32[2,1536]{1,0:T(2,128)S(1)}, f32[2,1536]{1,0:T(2,128)}, u32[]{:S(2)}) copy-start(f32[2,1536]{1,0:T(2,128)} %barrier_ref.1) | copy-start | bytes 36868
  0.7 0.7 copy-start.1
